TPU v7x, 32 devices: a whole 2x2x4 slice. The times are simulated.
32 devices in a mesh: shift: 2 (over y), expert: 4 (over z), shard: 4 (over x, core).
Axes of the slice: x: 2, y: 2, z: 4, core: 2. Of those that a mesh axis runs over, the one named last changes fastest.
Arguments:
- master_gate: float32 [128, 2048, 1024], P(('shift', 'expert'), 'shard'), parts along dimension 0, may hold values from -0.1875 to 0.1875
- master_up: float32 [128, 2048, 1024], P(('shift', 'expert'), 'shard'), parts along dimension 0, may hold values from -0.1875 to 0.1875
- router_weight: float32 [4096, 64], P(('shift', 'shard'), 'expert'), parts along dimension 0, may hold values from -0.125 to 0.125
- router_gain: float32 [4096], P(('shift', 'shard')), parts along dimension 0, may hold values from 0.25 to 1.75
Outputs:
- final_gate: bfloat16 [128, 2048, 1024], P(('shift', 'expert'), None, 'shard'), parts along dimension 0
- final_up: bfloat16 [128, 2048, 1024], P(('shift', 'expert'), None, 'shard'), parts along dimension 0
- scale_gate: float32 [128, 1024], P(('shift', 'expert'), 'shard'), parts along dimension 0
- scale_up: float32 [128, 1024], P(('shift', 'expert'), 'shard'), parts along dimension 0
- serve_router: bfloat16 [4096, 64], P('shift'), parts along dimension 0
There are 2 independent parts, one for each index of `shift`. A program takes and returns all parts, laid end to end along the dimension named above; each array names one. Nothing has to cross between parts.
All inputs are finite; a program needn't handle non-finite values. Where the computation divides by a largest or mean magnitude, that divisor is 1e-20 or more.
Results may differ from a plain program's by a relative error of at most 0.001.
Values may be sent and summed in bfloat16 or wider, within the bound.
A program may use at most 256 MiB of HBM per device.

v0:
```python
import jax
import jax.numpy as jnp
from jax import lax
from jax.sharding import PartitionSpec as P


def shards(master_gate, master_up, router_weight, router_gain):
    scale_gate, scale_up = lax.pmax(
        (jnp.max(jnp.abs(master_gate), axis=1), jnp.max(jnp.abs(master_up), axis=1)), "shard"
    )
    narrow_gate, narrow_up = (
        (master_gate / jnp.expand_dims(scale_gate, 1)).astype(jnp.bfloat16),
        (master_up / jnp.expand_dims(scale_up, 1)).astype(jnp.bfloat16),
    )
    final_gate, final_up = (
        lax.all_to_all(narrow_gate, "shard", split_axis=2, concat_axis=1, tiled=True),
        lax.all_to_all(narrow_up, "shard", split_axis=2, concat_axis=1, tiled=True),
    )
    scale_gate = lax.dynamic_slice_in_dim(
        scale_gate, lax.axis_index("shard") * final_gate.shape[2], final_gate.shape[2], axis=1
    )
    scale_up = lax.dynamic_slice_in_dim(
        scale_up, lax.axis_index("shard") * final_up.shape[2], final_up.shape[2], axis=1
    )
    part_router = (router_weight * router_gain[:, None]).astype(jnp.bfloat16)
    row_router = lax.all_gather(part_router, "shard", axis=0, tiled=True)
    serve_router = lax.all_gather(row_router, "expert", axis=1, tiled=True)
    return (final_gate, final_up, scale_gate, scale_up, serve_router)


def solution(mesh):
    in_specs = (
        P(("shift", "expert"), "shard", None),
        P(("shift", "expert"), "shard", None),
        P(("shift", "shard"), "expert"),
        P(("shift", "shard")),
    )
    out_specs = (
        P(("shift", "expert"), None, "shard"),
        P(("shift", "expert"), None, "shard"),
        P(("shift", "expert"), "shard"),
        P(("shift", "expert"), "shard"),
        P("shift", None),
    )
    return jax.shard_map(shards, mesh=mesh, in_specs=in_specs, out_specs=out_specs, check_vma=False)
```

profile of v0, /device:TPU:0, one launch (start us, length us, event | category | flops | bytes accessed | tf_op | source)
XLA Modules:
  0.0 541.3 jit_solution(9778503414393642907)
XLA Ops:
  7.2 0.0 all-reduce.3.cloned.1.call-start
  7.2 0.0 copy-start
  7.2 12.6 %abs_reduce_fusion = f32[16,1024]{1,0:T(8,128)} fusion(f32[16,512,1024]{2,1,0:T(8,128)} %param.5), kind=kLoop, calls=%fused_computation.1 | loop fusion | flops 16760832 | bytes 33619968 | tf_op jit(solution)/shard_map/reduce_max | solution.py:9
  19.8 7.6 %copy-done = f32[16,512,1024]{2,1,0:T(8,128)S(1)} copy-done((f32[16,512,1024]{2,1,0:T(8,128)S(1)}, f32[16,512,1024]{2,1,0:T(8,128)}, u32[]{:S(2)}) %copy-start) | copy-done | bytes 33554456
  27.4 2.7 abs_reduce_fusion.1
  30.1 0.0 all-reduce.3.cloned.1.call-update
  30.2 34.2 %copy.12 = f32[16,512,1024]{1,0,2:T(8,128)} copy(f32[16,512,1024]{2,1,0:T(8,128)} %param.4) | data formatting | bytes 67108864 | tf_op args[0]
  64.4 0.5 all-reduce.3.cloned.1.call-done
  64.9 1.0 copy.11
  66.0 17.7 %divide_convert_fusion.1 = bf16[16,512,1024]{1,0,2:T(8,128)(2,1)} fusion(f32[16,512,1024]{1,0,2:T(8,128)} %copy.12, f32[16,1024]{0,1:T(8,128)S(1)} %copy.11), kind=kLoop, calls=%fused_computation.2 | loop fusion | flops 16777216 | bytes 50397184 | tf_op jit(solution)/shard_map/convert_element_type | solution.py:12
  83.6 7.1 %all-to-all-start = ((bf16[16,512,1024]{1,0,2:T(8,128)(2,1)}), bf16[16,512,1024]{1,0,2:T(8,128)(2,1)}, u32[]{:S(2)}, u32[]{:S(2)}) async-start(bf16[16,512,1024]{1,0,2:T(8,128)(2,1)} %divide_convert_fusion.1), calls=%async_computation | async-start | bytes 33554432 | tf_op jit(solution)/shard_map/all_to_all | solution.py:16
  90.7 0.0 copy-start.1
  90.7 34.2 %copy.15 = f32[16,512,1024]{1,0,2:T(8,128)} copy(f32[16,512,1024]{2,1,0:T(8,128)} %param.5) | data formatting | bytes 67108864 | tf_op args[1]
  124.9 0.0 copy-done.1
  124.9 0.2 copy.14
  125.1 0.0 copy-start.2
  125.1 0.0 copy-start.3
  125.2 17.7 %divide_convert_fusion = bf16[16,512,1024]{1,0,2:T(8,128)(2,1)} fusion(f32[16,512,1024]{1,0,2:T(8,128)} %copy.15, f32[16,1024]{0,1:T(8,128)S(1)} %copy.14), kind=kLoop, calls=%fused_computation | loop fusion | flops 16777216 | bytes 50397184 | tf_op jit(solution)/shard_map/convert_element_type | solution.py:13
  142.8 131.1 %all-to-all-done = bf16[16,512,1024]{1,0,2:T(8,128)(2,1)} async-done(((bf16[16,512,1024]{1,0,2:T(8,128)(2,1)}), bf16[16,512,1024]{1,0,2:T(8,128)(2,1)}, u32[]{:S(2)}, u32[]{:S(2)}) %all-to-all-start) | async-done | bytes 16777248 | tf_op jit(solution)/shard_map/all_to_all | solution.py:16
  273.9 7.0 %all-to-all-start.1 = ((bf16[16,512,1024]{1,0,2:T(8,128)(2,1)}), bf16[16,512,1024]{1,0,2:T(8,128)(2,1)}, u32[]{:S(2)}, u32[]{:S(2)}) async-start(bf16[16,512,1024]{1,0,2:T(8,128)(2,1)} %divide_convert_fusion), calls=%async_computation.1 | async-start | bytes 33554432 | tf_op jit(solution)/shard_map/all_to_all | solution.py:17
  280.9 0.0 copy-done.2
  280.9 0.0 copy-done.3
  280.9 184.1 %all_gather.6 = bf16[2048,16]{0,1:T(8,128)(2,1)S(1)} all-gather(bf16[512,16]{0,1:T(8,128)(2,1)S(1)} %multiply_convert_fusion), channel_id=1, replica_groups=mesh['shift'=2,'expert'=4,'shard'=4] {'shard'}, dimensions={0}, use_global_device_ids=true | all-gather | bytes 81920 | tf_op jit(solution)/shard_map/all_gather | solution.py:26
  465.0 15.1 %all_gather.7 = bf16[2048,64]{0,1:T(8,128)(2,1)S(1)} all-gather(bf16[2048,16]{0,1:T(8,128)(2,1)S(1)} %all_gather.6), channel_id=1, replica_groups=mesh['shift'=2,'expert'=4,'shard'=4] {'expert'}, dimensions={1}, use_global_device_ids=true | all-gather | bytes 327680 | tf_op jit(solution)/shard_map/all_gather | solution.py:27
  480.1 1.3 constant_dynamic-slice_fusion
  481.4 26.2 %copy.13 = bf16[16,4,512,256]{3,2,1,0:T(8,128)(2,1)} copy(bf16[16,4,512,256]{2,0,3,1:T(8,128)(2,1)} %bitcast.1) | data formatting | bytes 33554432 | tf_op jit(solution)/shard_map/all_to_all | solution.py:16
  507.6 0.0 all-to-all-done.1
  507.6 26.2 %copy.16 = bf16[16,4,512,256]{3,2,1,0:T(8,128)(2,1)} copy(bf16[16,4,512,256]{2,0,3,1:T(8,128)(2,1)} %bitcast.4) | data formatting | bytes 33554432 | tf_op jit(solution)/shard_map/all_to_all | solution.py:17
  533.8 0.7 copy.20
  (1 shorter events, 0.0 us)
Async XLA Ops:
  7.2 57.7 %all-reduce.3.cloned.1.call-start = ((), (), s32[]{:S(2)}) async-start(), calls=%async_computation.2 | async-start | bytes 262144 | tf_op jit(solution)/shard_map/pmax | solution.py:8
  7.2 20.2 %copy-start = (f32[16,512,1024]{2,1,0:T(8,128)S(1)}, f32[16,512,1024]{2,1,0:T(8,128)}, u32[]{:S(2)}) copy-start(f32[16,512,1024]{2,1,0:T(8,128)} %param.4) | copy-start | bytes 100663296
  83.6 190.3 %all-to-all-start = ((bf16[16,512,1024]{1,0,2:T(8,128)(2,1)}), bf16[16,512,1024]{1,0,2:T(8,128)(2,1)}, u32[]{:S(2)}, u32[]{:S(2)}) async-start(bf16[16,512,1024]{1,0,2:T(8,128)(2,1)} %divide_convert_fusion.1), calls=%async_computation | async-start | bytes 33554432 | tf_op jit(solution)/shard_map/all_to_all | solution.py:16
  90.7 34.2 %copy-start.1 = (f32[16,1024]{1,0:T(8,128)S(1)}, f32[16,1024]{1,0:T(8,128)}, u32[]{:S(2)}) copy-start(f32[16,1024]{1,0:T(8,128)} %get-tuple-element.6) | copy-start | bytes 196612
  125.1 155.7 %copy-start.2 = (f32[512,16]{0,1:T(8,128)S(1)}, f32[512,16]{0,1:T(8,128)}, u32[]{:S(2)}) copy-start(f32[512,16]{0,1:T(8,128)} %param.6) | copy-start | bytes 98308
  125.1 155.7 %copy-start.3 = (f32[512]{0:T(512)S(1)}, f32[512]{0:T(512)}, u32[]{:S(2)}) copy-start(f32[512]{0:T(512)} %param.7) | copy-start | bytes 6148
  273.9 233.7 %all-to-all-start.1 = ((bf16[16,512,1024]{1,0,2:T(8,128)(2,1)}), bf16[16,512,1024]{1,0,2:T(8,128)(2,1)}, u32[]{:S(2)}, u32[]{:S(2)}) async-start(bf16[16,512,1024]{1,0,2:T(8,128)(2,1)} %divide_convert_fusion), calls=%async_computation.1 | async-start | bytes 33554432 | tf_op jit(solution)/shard_map/all_to_all | solution.py:17
Sparse Core Ops, SparseCore 0:
  30.3 34.5 all-reduce.2
where the time goes:
time: 544 us; the launch traced here: 541 us
  blocking collectives  199 us (37%)
  local copies, waits for them, and re-layouts  132 us (24%)
  waiting for transfers between devices  132 us (24%)
  other arithmetic  50.7 us (9%)
  starting transfers between devices  14.1 us (3%)
  between operations  14.1 us (3%)
    all_gather x1, blocking collectives, shards(): row_router = lax.all_gather(part_router, 'shard', axis=0, tiled=True)  184 us
    all_to_all x1, waiting for transfers between devices, shards(): lax.all_to_all(narrow_gate, 'shard', split_axis=2, concat_axis=1, tiled=T...  131 us
    unnamed x11, local copies, waits for them, and re-layouts  76.7 us
    all_to_all x1, local copies, waits for them, and re-layouts, shards(): lax.all_to_all(narrow_up, 'shard', split_axis=2, concat_axis=1, tiled=True)  26.2 us
    all_to_all x1, local copies, waits for them, and re-layouts, shards(): lax.all_to_all(narrow_gate, 'shard', split_axis=2, concat_axis=1, tiled=T...  26.2 us
    convert_element_type x1, other arithmetic, shards(): (master_gate / jnp.expand_dims(scale_gate, 1)).astype(jnp.bfloat16)  17.7 us
    convert_element_type x1, other arithmetic, shards(): (master_up / jnp.expand_dims(scale_up, 1)).astype(jnp.bfloat16)  17.7 us
    all_gather x1, blocking collectives, shards(): serve_router = lax.all_gather(row_router, 'expert', axis=1, tiled=True)  15.1 us
  transfers between devices with their start and end apart: 3, of which 2 were waited for; matrix products, arithmetic and copies ran while one was open for 21% of the time, Pallas kernels for 0%

commit v1 on v0

v1 whole, which is shorter than its diff:
```python
import functools

import jax
import jax.numpy as jnp
from jax import lax
from jax.experimental import pallas as pl
from jax.experimental.pallas import tpu as pltpu
from jax.sharding import PartitionSpec as P

MESH = pl.DeviceIdType.MESH
LANES = 128
LAG = 6
AHEAD = 2
SLOTS = 5


def exchange(
    n, groups, gate, up, router, narrow, tail, scales, routers, held, out, mine, theirs,
    load_sem, max_send, max_recv, send_sem, recv_sem, keep_sem, rt_send, rt_recv, rt_keep,
):
    me, group = lax.axis_index("shard"), lax.axis_index("expert")
    items, rows, width, depth = 2 * gate.shape[0], gate.shape[1], out.shape[3], held.shape[0]
    blocks, per = gate.shape[2] // LANES, width // LANES
    others = [(j, g) for g in range(groups) for j in range(n) if (j, g) != (0, 0)]

    def peer(j):
        return lax.rem(me + j, n)

    def device(j, g):
        return {"shard": peer(j), "expert": lax.rem(group + g, groups)}

    def load(k):
        slot, expert = lax.rem(k, depth), k // 2

        @pl.when(lax.rem(k, 2) == 0)
        def _():
            pltpu.make_async_copy(gate.at[expert], held.at[slot], load_sem.at[slot]).start()

        @pl.when(lax.rem(k, 2) == 1)
        def _():
            pltpu.make_async_copy(up.at[expert], held.at[slot], load_sem.at[slot]).start()

    def send_max(k, j):
        return pltpu.make_async_remote_copy(
            mine.at[k], theirs.at[k, j - 1], max_send, max_recv.at[k],
            device_id=device(j, 0), device_id_type=MESH,
        )

    def place(k):
        return narrow.at[lax.rem(k, 2), k // 2, pl.ds(pl.multiple_of(me * rows, rows), rows)]

    def send(k, j):
        slot = lax.rem(k, SLOTS)
        return pltpu.make_async_remote_copy(
            out.at[slot, peer(j)], place(k), send_sem.at[slot], recv_sem.at[j - 1],
            device_id=device(j, 0), device_id_type=MESH,
        )

    def keep(k):
        slot = lax.rem(k, SLOTS)
        return pltpu.make_async_copy(out.at[slot, me], place(k), keep_sem.at[slot])

    def leave(k):
        slot = lax.rem(k, SLOTS)
        return pltpu.make_async_copy(out.at[slot], tail.at[:, lax.rem(k, 2)], keep_sem.at[slot])

    def sent(k):
        slot = lax.rem(k, SLOTS)
        ref = out.at[slot, pl.ds(0, n - 1)]
        pltpu.make_async_copy(ref, ref, send_sem.at[slot]).wait()
        keep(k).wait()

    for k in range(AHEAD):
        load(jnp.int32(k))
    barrier = pltpu.get_barrier_semaphore()
    for j, g in others:
        pl.semaphore_signal(barrier, inc=1, device_id=device(j, g), device_id_type=MESH)
    pl.semaphore_wait(barrier, len(others))

    home = routers.at[group * n + me]
    for j, g in others:
        pltpu.make_async_remote_copy(
            router, home, rt_send, rt_recv, device_id=device(j, g), device_id_type=MESH
        ).start()
    own = pltpu.make_async_copy(router, home, rt_keep)
    own.start()

    def step(k, _):
        @pl.when(k + AHEAD < items)
        def _():
            load(k + AHEAD)

        @pl.when(k < items)
        def _():
            slot = lax.rem(k, depth)
            pltpu.make_async_copy(gate.at[0], held.at[slot], load_sem.at[slot]).wait()
            for b in range(blocks):
                column = held[slot, :, b * LANES : (b + 1) * LANES]
                mine[k, b : b + 1, :] = jnp.max(jnp.abs(column), axis=0, keepdims=True)
            for j in range(1, n):
                send_max(k, j).start()

        q = k - LAG

        @pl.when(q >= 0)
        def _():
            @pl.when(q >= SLOTS)
            def _():
                sent(q - SLOTS)

            pltpu.make_async_copy(theirs.at[q], theirs.at[q], max_recv.at[q]).wait()
            scale = mine[q]
            for j in range(1, n):
                scale = jnp.maximum(scale, theirs[q, j - 1])
            scales[q] = scale
            slot, source = lax.rem(q, SLOTS), lax.rem(q, depth)
            for b in range(blocks):
                at = (b % per) * LANES
                column = held[source, :, b * LANES : (b + 1) * LANES]
                out[slot, b // per, :, at : at + LANES] = (column / scale[b : b + 1]).astype(
                    jnp.bfloat16
                )

            @pl.when(q < items - 2)
            def _():
                for j in range(1, n):
                    send(q, j).start()
                keep(q).start()

            @pl.when(q >= items - 2)
            def _():
                leave(q).start()

        return 0

    lax.fori_loop(0, items + LAG, step, 0)

    def drain(k, _):
        sent(k)
        return 0

    lax.fori_loop(items - SLOTS, items - 2, drain, 0)
    for k in (items - 2, items - 1):
        leave(jnp.int32(k)).wait()
    pltpu.make_async_copy(theirs, theirs, max_send).wait()
    for j in range(1, n):
        ref = narrow.at[:, :, pl.ds(pl.multiple_of(peer(n - j) * rows, rows), rows)]
        pltpu.make_async_copy(ref, ref, recv_sem.at[j - 1]).wait()
    rest = routers.at[pl.ds(0, n * groups - 1)]
    pltpu.make_async_copy(rest, rest, rt_send).wait()
    pltpu.make_async_copy(rest, rest, rt_recv).wait()
    own.wait()


def spread(narrow, gate, up):
    gate[...] = narrow[0]
    up[...] = narrow[1]


def finish(arrived, gate_in, up_in, gate, up):
    gate[...] = arrived[:, 0]
    up[...] = arrived[:, 1]


def by_kernel(n, groups, gate, up, router, gain):
    experts, rows, columns = gate.shape
    width, items, depth = columns // n, 2 * experts, LAG + AHEAD + 1
    tokens, share = router.shape
    part = (router * gain[:, None]).astype(jnp.bfloat16).reshape(-1, LANES)
    anywhere = pl.BlockSpec(memory_space=pl.ANY)
    inside = pl.BlockSpec(memory_space=pltpu.VMEM)
    dma = pltpu.SemaphoreType.DMA
    narrow, tail, scales, routers = pl.pallas_call(
        functools.partial(exchange, n, groups),
        name="exchange",
        out_shape=(
            jax.ShapeDtypeStruct((2, experts - 1, n * rows, width), jnp.bfloat16),
            jax.ShapeDtypeStruct((n, 2, rows, width), jnp.bfloat16),
            jax.ShapeDtypeStruct((items, columns // LANES, LANES), jnp.float32),
            jax.ShapeDtypeStruct((groups * n,) + part.shape, jnp.bfloat16),
        ),
        in_specs=[anywhere, anywhere, inside],
        out_specs=(anywhere, anywhere, inside, anywhere),
        scratch_shapes=[
            pltpu.VMEM((depth, rows, columns), jnp.float32),
            pltpu.VMEM((SLOTS, n, rows, width), jnp.bfloat16),
            pltpu.VMEM((items, columns // LANES, LANES), jnp.float32),
            pltpu.VMEM((items, n - 1, columns // LANES, LANES), jnp.float32),
            dma((depth,)),
            dma,
            dma((items,)),
            dma((SLOTS,)),
            dma((n - 1,)),
            dma((SLOTS,)),
            dma,
            dma,
            dma,
        ],
        compiler_params=pltpu.CompilerParams(collective_id=0, has_side_effects=True),
    )(gate, up, part)
    arrived = lax.all_to_all(tail, "shard", split_axis=0, concat_axis=0, tiled=True)
    finals = (jax.ShapeDtypeStruct((experts, n * rows, width), jnp.bfloat16),) * 2
    most = pl.pallas_call(
        spread,
        name="spread",
        grid=(experts - 1,),
        out_shape=finals,
        in_specs=[pl.BlockSpec((2, 1, n * rows, width), lambda e: (0, e, 0, 0))],
        out_specs=(pl.BlockSpec((1, n * rows, width), lambda e: (e, 0, 0)),) * 2,
        cost_estimate=pl.CostEstimate(flops=0, bytes_accessed=4 * narrow.size, transcendentals=0),
    )(narrow)
    final_gate, final_up = pl.pallas_call(
        finish,
        name="finish",
        grid=(n,),
        out_shape=finals,
        in_specs=[
            pl.BlockSpec((1, 2, rows, width), lambda s: (s, 0, 0, 0)), anywhere, anywhere,
        ],
        out_specs=(pl.BlockSpec((1, rows, width), lambda s: (experts - 1, s, 0)),) * 2,
        input_output_aliases={1: 0, 2: 1},
    )(arrived, *most)
    scales = lax.dynamic_slice_in_dim(
        scales.reshape(experts, 2, columns), lax.axis_index("shard") * width, width, axis=2
    )
    serve_router = routers.reshape(groups, n * tokens, share).transpose(1, 0, 2)
    return (
        final_gate, final_up, scales[:, 0], scales[:, 1],
        serve_router.reshape(n * tokens, groups * share),
    )


def by_collectives(gate, up, router, gain):
    scale_gate, scale_up = lax.pmax(
        (jnp.max(jnp.abs(gate), axis=1), jnp.max(jnp.abs(up), axis=1)), "shard"
    )

    def serve(master, scale):
        narrow = (master / jnp.expand_dims(scale, 1)).astype(jnp.bfloat16)
        final = lax.all_to_all(narrow, "shard", split_axis=2, concat_axis=1, tiled=True)
        width = final.shape[2]
        return final, lax.dynamic_slice_in_dim(
            scale, lax.axis_index("shard") * width, width, axis=1
        )

    final_gate, scale_gate = serve(gate, scale_gate)
    final_up, scale_up = serve(up, scale_up)
    part = (router * gain[:, None]).astype(jnp.bfloat16)
    rows = lax.all_gather(part, "shard", axis=0, tiled=True)
    return final_gate, final_up, scale_gate, scale_up, lax.all_gather(rows, "expert", axis=1, tiled=True)


def solution(mesh):
    n, groups = mesh.shape["shard"], mesh.shape["expert"]

    def shards(gate, up, router, gain):
        aligned = gate.shape[2] % (n * LANES) == 0 and gate.shape[1] % 16 == 0
        aligned = aligned and 2 * gate.shape[0] > SLOTS
        if n > 1 and aligned and router.size % (16 * LANES) == 0:
            return by_kernel(n, groups, gate, up, router, gain)
        return by_collectives(gate, up, router, gain)

    return jax.shard_map(
        shards,
        mesh=mesh,
        in_specs=(
            P(("shift", "expert"), "shard", None),
            P(("shift", "expert"), "shard", None),
            P(("shift", "shard"), "expert"),
            P(("shift", "shard")),
        ),
        out_specs=(
            P(("shift", "expert"), None, "shard"),
            P(("shift", "expert"), None, "shard"),
            P(("shift", "expert"), "shard"),
            P(("shift", "expert"), "shard"),
            P("shift", None),
        ),
        check_vma=False,
    )
```

time: 544 us -> 401 us (0.74)
  Pallas kernels: 0 us -> 385 us
  blocking collectives: 199 us -> 0 us
  waiting for transfers between devices: 132 us -> 0.01 us
  local copies, waits for them, and re-layouts: 132 us -> 9.82 us
  other arithmetic: 50.7 us -> 0.77 us
  between operations: 14.1 us -> 0.67 us
  starting transfers between devices: 14.1 us -> 3.62 us
    pallas_call x0 -> x3, Pallas kernels: none -> 385 us  [the longest x1 355 us: by_kernel(): pl.pallas_call(functools.partial(exchange, n, groups), name='exchange', o...]
    all_gather x2 -> x0, blocking collectives: 199 us -> none  [the longest x1 184 us: shards(): row_router = lax.all_gather(part_router, 'shard', axis=0, tiled=True)]
    all_to_all x2 -> x1, waiting for transfers between devices: 131 us -> 0.01 us  [by_kernel(): lax.all_to_all(tail, 'shard', split_axis=0, concat_axis=0, tiled=True)]
    unnamed x11 -> x2, local copies, waits for them, and re-layouts: 76.7 us -> 1.35 us
    all_to_all x2 -> x0, local copies, waits for them, and re-layouts: 52.3 us -> none  [the longest x1 26.2 us: shards(): lax.all_to_all(narrow_up, 'shard', split_axis=2, concat_axis=1, tiled=True)]
    convert_element_type x3 -> x1, other arithmetic: 35.3 us -> 0.77 us  [by_kernel(): part = (router * gain[:, None]).astype(jnp.bfloat16).reshape(-1, LANES)]
    reduce_max x2 -> x0, other arithmetic: 15.3 us -> none  [the longest x1 12.6 us: shards(): jnp.max(jnp.abs(master_up), axis=1)]
    all_to_all x2 -> x1, starting transfers between devices: 14.1 us -> 3.62 us  [by_kernel(): lax.all_to_all(tail, 'shard', split_axis=0, concat_axis=0, tiled=True)]
  transfers between devices with their start and end apart: 3 -> 1, of which waited for: 2 -> 0; matrix products, arithmetic and copies ran while one was open for 21% -> 2% of each run, Pallas kernels for 0% -> 7%
where the time goes in v1:
time: 401 us; the launch traced here: 400 us
  Pallas kernels  385 us (96%)
  local copies, waits for them, and re-layouts  9.82 us (2%)
    pallas_call x1, Pallas kernels, by_kernel(): pl.pallas_call(functools.partial(exchange, n, groups), name='exchange', o...  355 us
    pallas_call x1, Pallas kernels, by_kernel(): pl.pallas_call(spread, name='spread', grid=(experts - 1,), out_shape=fina...  26.5 us
  transfers between devices with their start and end apart: 1, of which 0 were waited for; matrix products, arithmetic and copies ran while one was open for 2% of the time, Pallas kernels for 7%

profile of v1, /device:TPU:0, one launch (start us, length us, event | category | flops | bytes accessed | tf_op | source)
XLA Modules:
  0.0 399.7 jit_solution(11008754689263267707)
XLA Ops:
  0.6 0.8 multiply_convert_fusion
  1.4 0.1 copy.16
  1.5 0.7 reshape.23.router
  2.3 354.6 %exchange.1 = (bf16[2,15,2048,256]{3,2,1,0:T(8,128)(2,1)}, bf16[4,2,512,256]{3,2,1,0:T(8,128)(2,1)}, f32[32,8,128]{2,1,0:T(8,128)}, bf16[16,64,128]{2,1,0:T(8,128)(2,1)}) custom-call(f32[16,512,1024]{2,1,0:T(8,128)} %gate.1, f32[16,512,1024]{2,1,0:T(8,128)} %up.1, bf16[64,128]{1,0:T(8,128)(2,1)} %reshape.23.router), custom_call_target="tpu_custom_call" | custom-call | tf_op jit(solution)/shard_map/exchange/pallas_call | solution.py:173
  356.8 3.6 all-to-all-start
  360.5 1.0 reshape.24
  361.4 3.4 reshape.25
  364.9 2.5 copy.18
  367.4 26.5 %spread.1 = (bf16[16,2048,256]{2,1,0:T(8,128)(2,1)}, bf16[16,2048,256]{2,1,0:T(8,128)(2,1)}) custom-call(bf16[2,15,2048,256]{3,2,1,0:T(8,128)(2,1)} %get-tuple-element.14.narrow), custom_call_target="tpu_custom_call" | custom-call | bytes 62914560 | tf_op jit(solution)/shard_map/spread/pallas_call | solution.py:203
  393.9 0.1 constant_dynamic-slice_fusion.1
  394.0 0.6 copy_bitcast_fusion
  394.6 0.0 all-to-all-done.arrived
  394.6 0.0 copy-start
  394.6 1.3 copy-done
  396.0 3.8 finish.1
Async XLA Ops:
  356.8 37.8 %all-to-all-start = ((bf16[4,2,512,256]{3,2,1,0:T(8,128)(2,1)}), bf16[4,2,512,256]{3,2,1,0:T(8,128)(2,1)S(1)}, u32[]{:S(2)}, u32[]{:S(2)}) async-start(bf16[4,2,512,256]{3,2,1,0:T(8,128)(2,1)} %get-tuple-element.13), calls=%async_computation | async-start | bytes 4194304 | tf_op jit(solution)/shard_map/all_to_all | solution.py:201
  394.6 1.3 copy-start
